TPU v7x, 32 devices: a whole 2x2x4 slice. The times are simulated.
32 devices in a mesh: row: 8 (over y, x, core), col: 4 (over z).
Axes of the slice: x: 2, y: 2, z: 4, core: 2. Of those that a mesh axis runs over, the one named last changes fastest.
Arguments:
- tiles: float32 [8, 4, 4, 512, 512], P('row', 'col'), may hold values from 0 to 16777212, as said below
- tile_index: int32 [8, 4, 4, 2], P('row', 'col'), may hold values from 0 to 3, as said below
- tile_count: int32 [8, 4], P('row', 'col'), may hold values from 0 to 4, as said below
- iterate: float32 [8192, 32], P(('row', 'col')), may hold values from 0 to 16777212, as said below
- basis: float32 [8192, 32], P(('row', 'col')), may hold values from 0 to 16777212, as said below
- coefficients: float32 [256, 32, 32], P(('row', 'col')), may hold values from 0 to 16777212, as said below
- start_degree: int32 [1], replicated, may hold values from 1 to 255
Outputs:
- scaled_iterate: float32 [8192, 32], P(('row', 'col'))
Inputs may be any that keep to these rules, and one draw needn't show every extreme that they name: `tiles`: integers 0 to 16777212. `iterate`: integers 0 to 16777212. `basis`: integers 0 to 16777212. `coefficients`: integers 0 to 16777212. tile_index[..., 0] lies in 0 to 1 and tile_index[..., 1] in 0 to 3; the 4 slots of one device name distinct tiles, unoccupied slots included; unoccupied slots hold arbitrary entries. `tile_count`: some device has 4 occupied slots.
All inputs are finite; a program needn't handle non-finite values.
Results may differ from a plain program's by a relative error of at most 0.0003.
Values sent between devices are 32-bit elements; how exact they have to be, the bound alone decides.
A program may use at most 64 MiB of HBM per device.

v0:
```python
import jax
import jax.numpy as jnp
from jax import lax
from jax.sharding import PartitionSpec as P

STEPS = 2


PRIME = 16777213
RADIX = 16777216


def from_root(block, axis, source):
    block = jnp.where(lax.axis_index(axis) == source, block, jnp.zeros_like(block))
    return lax.psum(block, axis)


def fold_word(value):
    value = value % RADIX + 3 * (value // RADIX)
    return jnp.where(value >= PRIME, value - PRIME, value)


def add_mod(first, second):
    total = first + second
    return jnp.where(total >= PRIME, total - PRIME, total)


def shift_mod(value, shift):
    while shift > 0:
        amount = min(shift, 7)
        value = fold_word(value * 2**amount)
        shift = shift - amount
    return value


def split_limbs(values, bits, count):
    whole = values.astype(jnp.int32)
    return [(whole // 2 ** (bits * place) % 2**bits).astype(jnp.bfloat16) for place in range(count)]


def combine_limbs(product, left_bits, right_bits, width):
    whole = product.astype(jnp.int32)
    total = None
    for left in range(whole.shape[-3]):
        for right in range(whole.shape[-1] // width):
            piece = whole[..., left, :, right * width : (right + 1) * width]
            term = shift_mod(piece, left_bits * left + right_bits * right)
            total = term if total is None else add_mod(total, term)
    return total


def tile_products(tile_limbs, gathered, column_slots, tile):
    column_limbs = jnp.concatenate(split_limbs(gathered, 6, 4), axis=1)
    windows = jax.vmap(
        lambda column: lax.dynamic_slice_in_dim(column_limbs, column * tile, tile, 0)
    )(column_slots)
    product = jnp.einsum("tlik,tkc->tlic", tile_limbs, windows, preferred_element_type=jnp.float32)
    return combine_limbs(product, 8, 6, gathered.shape[1])


def on_device(tiles, tile_index, tile_count, iterate, basis, coefficients, start_degree):
    block = tiles[0, 0]
    tile = block.shape[-1]
    slots = block.shape[0]
    rows_dev = iterate.shape[0]
    width = iterate.shape[1]
    count_col = lax.axis_size("col")
    block_rows = rows_dev * count_col // tile
    per_device = coefficients.shape[0]
    tile_limbs = jnp.stack(split_limbs(block, 8, 3), axis=1)
    row_slots = tile_index[0, 0, :, 0]
    column_slots = tile_index[0, 0, :, 1]
    used = jnp.arange(slots) < tile_count[0, 0]
    match = row_slots[:, None] == jnp.arange(block_rows)[None, :]
    basis_limbs = jnp.stack(split_limbs(basis, 8, 3))
    degree = start_degree[0]
    current = iterate
    for step in range(STEPS):
        wanted = degree - step
        holding = lax.dynamic_index_in_dim(coefficients, wanted % per_device, 0, keepdims=False)
        coef = from_root(holding, ("row", "col"), wanted // per_device)
        packed = lax.all_gather(current.reshape(-1, 128), "row", axis=0, tiled=True)
        gathered = packed.reshape(-1, width)
        residues = tile_products(tile_limbs, gathered, column_slots, tile)
        kept = jnp.where(used[:, None, None], residues, 0)
        partial_value = (
            jnp.sum(jnp.where(match[:, :, None, None], kept[:, None], 0), axis=0) % PRIME
        )
        partial_value = partial_value.reshape(block_rows * tile, width)
        pieces = partial_value.astype(jnp.float32).reshape(count_col, -1, 128)
        arrived = lax.all_to_all(pieces, "col", split_axis=0, concat_axis=0, tiled=True)
        local = (jnp.sum(arrived.astype(jnp.int32), axis=0) % PRIME).reshape(rows_dev, width)
        coef_limbs = jnp.concatenate(split_limbs(coef, 8, 3), axis=1)
        basis_product = jnp.einsum(
            "lrk,kc->lrc", basis_limbs, coef_limbs, preferred_element_type=jnp.float32
        )
        basis_term = combine_limbs(basis_product, 8, 8, width)
        current = add_mod(local, basis_term).astype(jnp.float32)
    return current / PRIME


def solution(mesh):
    in_specs = (
        P("row", "col", None, None, None),
        P("row", "col", None, None),
        P("row", "col"),
        P(("row", "col"), None),
        P(("row", "col"), None),
        P(("row", "col"), None, None),
        P(),
    )
    out_specs = P(("row", "col"), None)
    return jax.shard_map(
        on_device, mesh=mesh, in_specs=in_specs, out_specs=out_specs, check_vma=False
    )
```

profile of v0, /device:TPU:0, one launch (start us, length us, event | category | flops | bytes accessed | tf_op | source)
XLA Modules:
  0.0 145.7 jit_solution(8975279407004597319)
XLA Ops:
  1.4 11.8 %fusion = (bf16[4,1,512,512]{3,2,1,0:T(8,128)(2,1)S(1)}, bf16[4,1,512,512]{3,2,1,0:T(8,128)(2,1)}, bf16[4,1,512,512]{3,2,1,0:T(8,128)(2,1)}) fusion(f32[1,1,4,512,512]{4,3,2,1,0:T(8,128)} %param.7), kind=kLoop, calls=%fused_computation.19 | loop fusion | flops 57671680 | bytes 10485760 | tf_op jit(solution)/shard_map/convert_element_type | solution.py:38
  13.3 11.0 %all_gather.6 = f32[512,128]{1,0:T(8,128)S(1)} all-gather(f32[64,128]{1,0:T(8,128)S(1)} %reshape.310), channel_id=1, replica_groups=mesh['row'=8,'col'=4] {'row'}, dimensions={0}, use_global_device_ids=true | all-gather | bytes 294912 | tf_op jit(solution)/shard_map/all_gather | solution.py:82
  24.6 3.1 %fusion.13 = (bf16[2048,32]{1,0:T(8,128)(2,1)S(1)}, bf16[2048,32]{1,0:T(8,128)(2,1)S(1)}, bf16[2048,32]{1,0:T(8,128)(2,1)S(1)}, bf16[2048,32]{1,0:T(8,128)(2,1)S(1)}) fusion(s32[2048,32]{1,0:T(8,128)S(1)} %convert_element_type.162), kind=kLoop, calls=%fused_computation.76 | loop fusion | flops 4980736 | bytes 786432 | tf_op jit(solution)/shard_map/convert_element_type | solution.py:38
  28.4 5.7 %while.2 = (s32[]{:T(128)}, bf16[2048,128]{1,0:T(8,128)(2,1)S(1)}, s32[4,2]{0,1:T(2,128)S(1)}, bf16[4,512,128]{2,1,0:T(8,128)(2,1)S(1)}, s32[]{:T(128)}) while((s32[]{:T(128)}, bf16[2048,128]{1,0:T(8,128)(2,1)S(1)}, s32[4,2]{0,1:T(2,128)S(1)}, bf16[4,512,128]{2,1,0:T(8,128)(2,1)S(1)}, s32[]{:T(128)}) %tuple.53), condition=%wide.while_cond, body=%wide.while_body.sunk | while | flops 2 | bytes 262249 | solution.py:55
  29.1 0.7 bitcast_dynamic-update-slice_fusion.4
  30.6 0.7 bitcast_dynamic-update-slice_fusion.4
  32.0 0.7 bitcast_dynamic-update-slice_fusion.4
  33.4 0.7 bitcast_dynamic-update-slice_fusion.4
  34.9 3.9 %fusion.11 = s32[4,3,512,128]{2,3,1,0:T(8,128)S(1)} fusion(bf16[4,1,512,512]{3,2,1,0:T(8,128)(2,1)} %get-tuple-element.40, bf16[4,1,512,512]{3,2,1,0:T(8,128)(2,1)} %get-tuple-element.41, bf16[4,1,512,512]{3,2,1,0:T(8,128)(2,1)S(1)} %get-tuple-element.39, bf16[4,512,128]{2,1,0:T(8,128)(2,1)S(1)} %get-tuple-element.12), kind=kOutput, calls=%fused_computation.32 | convolution fusion | flops 812384256 | bytes 9961472 | tf_op jit(solution)/shard_map/tlik,tkc->tlic/dot_general | solution.py:57
  38.9 9.4 %fusion.205 = s32[4,512,32]{1,2,0:T(8,128)S(1)} fusion(s32[4,3,512,128]{2,3,1,0:T(8,128)S(1)} %fusion.11, pred[4]{0:T(512)(128)(4,1)S(1)} %iota_compare_fusion.1), kind=kLoop, calls=%fused_computation.692 | loop fusion | flops 57016320 | bytes 3407876 | tf_op jit(solution)/shard_map/jit(_where)/broadcast_in_dim | solution.py:87
  49.5 4.9 %all-to-all-start = ((f32[4,64,128]{2,1,0:T(8,128)}), f32[4,64,128]{2,1,0:T(8,128)S(1)}, u32[]{:S(2)}, u32[]{:S(2)}) async-start(f32[4,64,128]{2,1,0:T(8,128)} %fusion.505), calls=%async_computation | async-start | bytes 262144 | tf_op jit(solution)/shard_map/all_to_all | solution.py:91
  56.0 40.0 %all-reduce.1 = (f32[32,32]{1,0:T(8,128)S(1)}, f32[32,32]{1,0:T(8,128)S(1)}) all-reduce(f32[32,32]{1,0:T(8,128)S(1)} %get-tuple-element.60, f32[32,32]{1,0:T(8,128)S(1)} %get-tuple-element.59), channel_id=1, replica_groups=mesh['row'=8,'col'=4] {'row','col'}, use_global_device_ids=true, to_apply=%region_2.3 | all-reduce | flops 2048 | bytes 16384 | tf_op jit(solution)/shard_map/psum | solution.py:15
  98.2 1.0 fusion.645
  99.2 10.3 %all_gather.7 = f32[512,128]{1,0:T(8,128)S(1)} all-gather(f32[64,128]{1,0:T(8,128)S(1)} %fusion.645), channel_id=1, replica_groups=mesh['row'=8,'col'=4] {'row'}, dimensions={0}, use_global_device_ids=true | all-gather | bytes 294912 | tf_op jit(solution)/shard_map/all_gather | solution.py:82
  109.8 3.1 %fusion.22 = (bf16[2048,32]{1,0:T(8,128)(2,1)S(1)}, bf16[2048,32]{1,0:T(8,128)(2,1)S(1)}, bf16[2048,32]{1,0:T(8,128)(2,1)S(1)}, bf16[2048,32]{1,0:T(8,128)(2,1)S(1)}) fusion(s32[2048,32]{1,0:T(8,128)S(1)} %convert_element_type.181), kind=kLoop, calls=%fused_computation.85 | loop fusion | flops 4980736 | bytes 786432 | tf_op jit(solution)/shard_map/convert_element_type | solution.py:38
  113.6 5.7 %while.3 = (s32[]{:T(128)}, bf16[2048,128]{1,0:T(8,128)(2,1)S(1)}, s32[4,2]{0,1:T(2,128)S(1)}, bf16[4,512,128]{2,1,0:T(8,128)(2,1)S(1)}, s32[]{:T(128)}) while((s32[]{:T(128)}, bf16[2048,128]{1,0:T(8,128)(2,1)S(1)}, s32[4,2]{0,1:T(2,128)S(1)}, bf16[4,512,128]{2,1,0:T(8,128)(2,1)S(1)}, s32[]{:T(128)}) %tuple.59), condition=%wide.while_cond.1, body=%wide.while_body.1.sunk | while | flops 2 | bytes 262249 | solution.py:55
  114.3 0.7 bitcast_dynamic-update-slice_fusion.5
  115.7 0.7 bitcast_dynamic-update-slice_fusion.5
  117.2 0.7 bitcast_dynamic-update-slice_fusion.5
  119.4 3.9 %fusion.12 = s32[4,3,512,128]{2,3,1,0:T(8,128)S(1)} fusion(bf16[4,1,512,512]{3,2,1,0:T(8,128)(2,1)} %get-tuple-element.40, bf16[4,1,512,512]{3,2,1,0:T(8,128)(2,1)} %get-tuple-element.41, bf16[4,1,512,512]{3,2,1,0:T(8,128)(2,1)S(1)} %get-tuple-element.39, bf16[4,512,128]{2,1,0:T(8,128)(2,1)S(1)} %get-tuple-element.20), kind=kOutput, calls=%fused_computation.33 | convolution fusion | flops 812384256 | bytes 9961472 | tf_op jit(solution)/shard_map/tlik,tkc->tlic/dot_general | solution.py:57
  123.3 9.4 %fusion.240 = s32[4,512,32]{1,2,0:T(8,128)S(1)} fusion(s32[4,3,512,128]{2,3,1,0:T(8,128)S(1)} %fusion.12, pred[4]{0:T(512)(128)(4,1)S(1)} %iota_compare_fusion.1), kind=kLoop, calls=%fused_computation.727 | loop fusion | flops 57016320 | bytes 3407876 | tf_op jit(solution)/shard_map/jit(_where)/broadcast_in_dim | solution.py:87
  134.0 3.5 %all-to-all-start.1 = ((f32[4,64,128]{2,1,0:T(8,128)}), f32[4,64,128]{2,1,0:T(8,128)S(1)}, u32[]{:S(2)}, u32[]{:S(2)}) async-start(f32[4,64,128]{2,1,0:T(8,128)} %fusion.506), calls=%async_computation.1 | async-start | bytes 262144 | tf_op jit(solution)/shard_map/all_to_all | solution.py:91
  137.8 6.1 %all-to-all-done.1 = f32[4,64,128]{2,1,0:T(8,128)S(1)} async-done(((f32[4,64,128]{2,1,0:T(8,128)}), f32[4,64,128]{2,1,0:T(8,128)S(1)}, u32[]{:S(2)}, u32[]{:S(2)}) %all-to-all-start.1) | async-done | bytes 131104 | tf_op jit(solution)/shard_map/all_to_all | solution.py:91
  144.1 1.6 %fusion.673 = f32[256,32]{0,1:T(8,128)} fusion(s32[256,32]{0,1:T(8,128)S(1)} %copy.44, s32[3,256,96]{1,2,0:T(8,128)S(1)} %convolution_convert_fusion), kind=kLoop, calls=%fused_computation.1601 | loop fusion | flops 5677056 | bytes 360448 | tf_op jit(solution)/shard_map/div | solution.py:99
  (76 shorter events, 15.7 us)
Async XLA Ops:
  1.4 11.8 %copy-start = (f32[256,32]{0,1:T(8,128)S(1)}, f32[256,32]{0,1:T(8,128)}, u32[]{:S(2)}) copy-start(f32[256,32]{0,1:T(8,128)} %param.10) | copy-start | bytes 98308
  38.8 16.2 %copy-start.1 = (f32[256,32]{0,1:T(8,128)S(1)}, f32[256,32]{0,1:T(8,128)}, u32[]{:S(2)}) copy-start(f32[256,32]{0,1:T(8,128)} %param.11) | copy-start | bytes 98308
  49.5 48.7 %all-to-all-start = ((f32[4,64,128]{2,1,0:T(8,128)}), f32[4,64,128]{2,1,0:T(8,128)S(1)}, u32[]{:S(2)}, u32[]{:S(2)}) async-start(f32[4,64,128]{2,1,0:T(8,128)} %fusion.505), calls=%async_computation | async-start | bytes 262144 | tf_op jit(solution)/shard_map/all_to_all | solution.py:91
  134.0 10.0 %all-to-all-start.1 = ((f32[4,64,128]{2,1,0:T(8,128)}), f32[4,64,128]{2,1,0:T(8,128)S(1)}, u32[]{:S(2)}, u32[]{:S(2)}) async-start(f32[4,64,128]{2,1,0:T(8,128)} %fusion.506), calls=%async_computation.1 | async-start | bytes 262144 | tf_op jit(solution)/shard_map/all_to_all | solution.py:91
where the time goes:
time: 146 us
  blocking collectives  61.2 us (42%)
  other arithmetic  44.1 us (30%)
  local copies, waits for them, and re-layouts  15.4 us (11%)
  matrix products  8.49 us (6%)
  starting transfers between devices  8.42 us (6%)
  waiting for transfers between devices  6.1 us (4%)
  between operations  1.76 us (1%)
    psum x1, blocking collectives, from_root(): return lax.psum(block, axis)  40 us
    all_gather x2, blocking collectives, on_device(): packed = lax.all_gather(current.reshape(-1, 128), 'row', axis=0, tiled=True)  21.3 us
    broadcast_in_dim x2, other arithmetic, on_device(): jnp.where(match[:, :, None, None], kept[:, None], 0)  18.8 us
    convert_element_type x4, other arithmetic, split_limbs(): (whole // 2 ** (bits * place) % 2 ** bits).astype(jnp.bfloat16)  18 us
    gather x24, local copies, waits for them, and re-layouts  11.3 us
    all_to_all x2, starting transfers between devices, on_device(): lax.all_to_all(pieces, 'col', split_axis=0, concat_axis=0, tiled=True)  8.42 us
    dot_general x2, matrix products, tile_products(): jnp.einsum('tlik,tkc->tlic', tile_limbs, windows, preferred_element_type=...  7.85 us
    all_to_all x2, waiting for transfers between devices, on_device(): lax.all_to_all(pieces, 'col', split_axis=0, concat_axis=0, tiled=True)  6.1 us
  transfers between devices with their start and end apart: 2, of which 1 were waited for; matrix products, arithmetic and copies ran while one was open for 2% of the time, Pallas kernels for 0%

commit v1 on v0

v1 whole, which is shorter than its diff:
```python
import functools

import jax
import jax.numpy as jnp
from jax import lax
from jax.experimental import pallas as pl
from jax.experimental.pallas import tpu as pltpu
from jax.sharding import PartitionSpec as P

STEPS = 2
PRIME = 16777213
HALF = 8388608.0
MAGIC = 12582912.0
LEFT = 3
RIGHT = 4
MESH = pl.DeviceIdType.MESH


def nearest(value):
    return (value + MAGIC) - MAGIC


def digits(value, bits, count):
    out = []
    for place in range(count - 1, 0, -1):
        top = nearest(value * (2.0 ** (-bits * place)))
        value = value - top * (2.0 ** (bits * place))
        out.append(top)
    out.append(value)
    return out[::-1]


def centred(value):
    return value - jnp.where(value > HALF, float(PRIME), 0.0)


def shrink(value):
    high = (value + 2**23) >> 24
    return value - (high << 24) + 3 * high


def shifted(value, shift):
    if shift == 0:
        return value
    return ((value & (2 ** (24 - shift) - 1)) << shift) + 3 * (value >> (24 - shift))


def kernel(
    n_row, n_col, index_ref, count_ref, degree_ref, tiles_ref, iterate_ref, basis_ref, coef_ref,
    out_ref, tbuf, abuf, gbuf, lbuf, wbuf, pbuf, rbuf, cur, bterm, csrc, crecv, fsum, frecv,
    tile_sem, ag_send, ag_recv, rs_send, rs_recv, ca_send, ca_recv, cb_send, cb_recv,
):
    me_row = lax.axis_index("row")
    me_col = lax.axis_index("col")
    slots, tile, _ = tiles_ref.shape
    width, rows_dev = iterate_ref.shape
    per_tile = tile // rows_dev
    block_rows = n_col // per_tile
    band = RIGHT * width

    def row_peer(d):
        return lax.rem(me_row + d, n_row)

    def col_peer(d):
        return lax.rem(me_col + d, n_col)

    loads = [
        pltpu.make_async_copy(tiles_ref.at[t], tbuf.at[t], tile_sem.at[t]) for t in range(slots)
    ]
    for load in loads:
        load.start()

    barrier = pltpu.get_barrier_semaphore()

    @pl.loop(1, n_row)
    def _(d):
        pl.semaphore_signal(barrier, inc=1, device_id={"row": row_peer(d)}, device_id_type=MESH)

    @pl.loop(1, n_col)
    def _(d):
        pl.semaphore_signal(barrier, inc=1, device_id={"col": col_peer(d)}, device_id_type=MESH)

    per_device = coef_ref.shape[0]
    me = me_row * n_col + me_col
    held = []
    for step in range(STEPS):
        wanted = degree_ref[0] - step
        matrix = coef_ref[lax.rem(wanted + per_device, per_device)]
        matrix = jnp.where(lax.div(wanted, per_device) == me, matrix, 0.0)
        held += [matrix[: width // 2], matrix[width // 2 :]]
    csrc[...] = jnp.concatenate(held, axis=1)

    pl.semaphore_wait(barrier, n_row + n_col - 2)

    def gather_copy(step, d, slot):
        return pltpu.make_async_remote_copy(
            src_ref=iterate_ref if step == 0 else cur,
            dst_ref=gbuf.at[step, slot],
            send_sem=ag_send.at[step, d],
            recv_sem=ag_recv.at[step, slot],
            device_id={"row": row_peer(d)},
            device_id_type=MESH,
        )

    def scatter_copy(step, chunk, slot, peer):
        return pltpu.make_async_remote_copy(
            src_ref=pbuf.at[step, chunk],
            dst_ref=rbuf.at[step, slot],
            send_sem=rs_send.at[step, chunk],
            recv_sem=rs_recv.at[step, slot],
            device_id={"col": peer},
            device_id_type=MESH,
        )

    def coef_col_copy(d, slot):
        return pltpu.make_async_remote_copy(
            src_ref=csrc,
            dst_ref=crecv.at[slot],
            send_sem=ca_send.at[d],
            recv_sem=ca_recv.at[slot],
            device_id={"col": col_peer(d)},
            device_id_type=MESH,
        )

    def coef_row_copy(d, slot):
        return pltpu.make_async_remote_copy(
            src_ref=fsum,
            dst_ref=frecv.at[slot],
            send_sem=cb_send.at[d],
            recv_sem=cb_recv.at[slot],
            device_id={"row": row_peer(d)},
            device_id_type=MESH,
        )

    def put_limbs(value, slot):
        parts = digits(centred(value), 6, RIGHT)
        lbuf[slot] = jnp.concatenate(parts, axis=0).astype(jnp.bfloat16)

    def split_tiles():
        rows = 64
        for t in range(slots):
            loads[t].wait()

            @pl.loop(0, tile // rows)
            def _(i, t=t):
                at = pl.ds(pl.multiple_of(i * rows, rows), rows)
                parts = digits(tbuf[t, at, :], 8, LEFT)
                for place in range(LEFT):
                    abuf[place, at, t * tile : (t + 1) * tile] = parts[place].astype(jnp.bfloat16)

    def basis_terms():
        @pl.loop(1, n_row)
        def _(d):
            src = lax.rem(me_row - d + n_row, n_row)
            coef_row_copy(d, src).wait_recv()

        def add(d, total):
            return total + frecv[lax.rem(me_row + d, n_row)]

        coefs = lax.fori_loop(1, n_row, add, fsum[...])
        basis_digits = [x.astype(jnp.bfloat16) for x in digits(centred(basis_ref[...]), 8, 3)]
        for step in range(STEPS):
            low = coefs[:, (2 * step) * width : (2 * step + 1) * width]
            high = coefs[:, (2 * step + 1) * width : (2 * step + 2) * width]
            matrix = centred(jnp.concatenate([low, high], axis=0))
            parts = [x.T.astype(jnp.bfloat16) for x in digits(matrix, 8, 3)]
            left = jnp.concatenate(parts, axis=0)
            sums = [None] * 5
            for place in range(3):
                product = jnp.dot(left, basis_digits[place], preferred_element_type=jnp.float32)
                for other in range(3):
                    piece = product[other * width : (other + 1) * width]
                    old = sums[place + other]
                    sums[place + other] = piece if old is None else old + piece
            sums = [x.astype(jnp.int32) for x in sums]
            total = sums[0] + 3 * sums[3] + ((sums[1] + 3 * sums[4]) << 8)
            total = total + shifted(sums[2], 16)
            bterm[step] = shrink(total)

    for step in range(STEPS):
        if step == 0:

            @pl.loop(1, n_col)
            def _(d):
                coef_col_copy(d, me_col).start()

        @pl.loop(1, n_row)
        def _(d, step=step):
            gather_copy(step, d, me_row).start()

        put_limbs((iterate_ref if step == 0 else cur)[...], me_row)
        if step == 0:
            split_tiles()

            def add_col(d, total):
                src = lax.rem(me_col - d + n_col, n_col)
                coef_col_copy(d, src).wait_recv()
                return total + crecv[src]

            fsum[...] = lax.fori_loop(1, n_col, add_col, csrc[...])

        @pl.loop(1, n_row)
        def _(d, step=step):
            src = lax.rem(me_row - d + n_row, n_row)
            gather_copy(step, d, src).wait_recv()
            put_limbs(gbuf[step, src], src)

        if step == 0:

            @pl.loop(1, n_row)
            def _(d):
                coef_row_copy(d, me_row).start()

        for t in range(slots):
            column = index_ref[t, 1]
            used = t < count_ref[0, 0]
            for part in range(per_tile):
                window = lbuf[column * per_tile + part]
                at = t * tile + part * rows_dev
                for a in range(block_rows):
                    keep = jnp.where(used & (index_ref[t, 0] == a), 1.0, 0.0).astype(jnp.bfloat16)
                    wbuf[a * band : (a + 1) * band, at : at + rows_dev] = window * keep

        for part in range(per_tile):
            rows = slice(part * rows_dev, (part + 1) * rows_dev)
            whole = [
                lax.dot_general(
                    wbuf[...],
                    abuf[place, rows, :],
                    (((1,), (1,)), ((), ())),
                    preferred_element_type=jnp.float32,
                ).astype(jnp.int32)
                for place in range(LEFT)
            ]
            for a in range(block_rows):
                total = None
                for j in range(RIGHT):
                    at = slice(a * band + j * width, a * band + (j + 1) * width)
                    p0, p1, p2 = [x[at] for x in whole]
                    term = p0 + ((p1 & 0xFFFF) << 8) + ((p2 & 0xFF) << 16)
                    term = shifted(term + 3 * ((p1 >> 16) + (p2 >> 8)), 6 * j)
                    total = term if total is None else total + term
                chunk = a * per_tile + part
                pbuf[step, chunk] = shrink(total).astype(jnp.float32)

                @pl.when(me_col != chunk)
                def _(step=step, chunk=chunk):
                    scatter_copy(step, chunk, me_col, chunk).start()

        if step == 0:
            basis_terms()

        def add_chunk(d, total, step=step):
            src = lax.rem(me_col - d + n_col, n_col)
            scatter_copy(step, src, src, src).wait_recv()
            return total + rbuf[step, src].astype(jnp.int32)

        start = bterm[step] + pbuf[step, me_col].astype(jnp.int32)
        value = shrink(lax.fori_loop(1, n_col, add_chunk, start))
        if step < STEPS - 1:
            cur[...] = value.astype(jnp.float32)
        else:
            value = jnp.where(value < 0, value + PRIME, value)
            out_ref[...] = value.astype(jnp.float32) / float(PRIME)

    @pl.loop(1, n_row)
    def _(d):
        for step in range(STEPS):
            gather_copy(step, d, me_row).wait_send()
        coef_row_copy(d, me_row).wait_send()

    @pl.loop(1, n_col)
    def _(d):
        for step in range(STEPS):
            scatter_copy(step, col_peer(d), me_col, col_peer(d)).wait_send()
        coef_col_copy(d, me_col).wait_send()


def on_device(tiles, tile_index, tile_count, iterate, basis, coefficients, start_degree):
    n_row = lax.axis_size("row")
    n_col = lax.axis_size("col")
    slots, tile = tiles.shape[2], tiles.shape[-1]
    rows_dev, width = iterate.shape
    block_rows = rows_dev * n_col // tile
    f32, bf16, dma = jnp.float32, jnp.bfloat16, pltpu.SemaphoreType.DMA
    vmem, smem = pltpu.VMEM, pltpu.SMEM
    out = pl.pallas_call(
        functools.partial(kernel, n_row, n_col),
        out_shape=jax.ShapeDtypeStruct((width, rows_dev), f32),
        in_specs=[pl.BlockSpec(memory_space=smem)] * 3
        + [pl.BlockSpec(memory_space=pl.ANY)]
        + [pl.BlockSpec(memory_space=vmem)] * 3,
        out_specs=pl.BlockSpec(memory_space=vmem),
        scratch_shapes=[
            vmem((slots, tile, tile), f32),
            vmem((LEFT, tile, slots * tile), bf16),
            vmem((STEPS, n_row, width, rows_dev), f32),
            vmem((n_row, RIGHT * width, rows_dev), bf16),
            vmem((block_rows * RIGHT * width, slots * tile), bf16),
            vmem((STEPS, n_col, width, rows_dev), f32),
            vmem((STEPS, n_col, width, rows_dev), f32),
            vmem((width, rows_dev), f32),
            vmem((STEPS, width, rows_dev), jnp.int32),
            vmem((width // 2, 2 * STEPS * width), f32),
            vmem((n_col, width // 2, 2 * STEPS * width), f32),
            vmem((width // 2, 2 * STEPS * width), f32),
            vmem((n_row, width // 2, 2 * STEPS * width), f32),
            dma((slots,)),
            dma((STEPS, n_row)),
            dma((STEPS, n_row)),
            dma((STEPS, n_col)),
            dma((STEPS, n_col)),
            dma((n_col,)),
            dma((n_col,)),
            dma((n_row,)),
            dma((n_row,)),
        ],
        compiler_params=pltpu.CompilerParams(
            collective_id=0, has_side_effects=True, vmem_limit_bytes=60 * 2**20
        ),
    )(tile_index[0, 0], tile_count, start_degree, tiles[0, 0], iterate.T, basis.T, coefficients)
    return out.T


def solution(mesh):
    in_specs = (
        P("row", "col", None, None, None),
        P("row", "col", None, None),
        P("row", "col"),
        P(("row", "col"), None),
        P(("row", "col"), None),
        P(("row", "col"), None, None),
        P(),
    )
    out_specs = P(("row", "col"), None)
    return jax.shard_map(
        on_device, mesh=mesh, in_specs=in_specs, out_specs=out_specs, check_vma=False
    )
```

time: 146 us -> 32.9 us (0.23)
  blocking collectives: 61.2 us -> 0 us
  other arithmetic: 44.1 us -> 0 us
  Pallas kernels: 0 us -> 28.6 us
  local copies, waits for them, and re-layouts: 15.4 us -> 2.71 us
  matrix products: 8.49 us -> 0 us
  starting transfers between devices: 8.42 us -> 0 us
  waiting for transfers between devices: 6.1 us -> 0 us
    psum x1 -> x0, blocking collectives: 40 us -> none  [from_root(): return lax.psum(block, axis)]
    pallas_call x0 -> x1, Pallas kernels: none -> 28.6 us  [on_device(): pl.pallas_call(functools.partial(kernel, n_row, n_col), out_shape=jax.Sha...]
    all_gather x2 -> x0, blocking collectives: 21.3 us -> none  [on_device(): packed = lax.all_gather(current.reshape(-1, 128), 'row', axis=0, tiled=True)]
    convert_element_type x9 -> x0, other arithmetic: 20.3 us -> none  [the longest x4 18 us: split_limbs(): (whole // 2 ** (bits * place) % 2 ** bits).astype(jnp.bfloat16)]
    broadcast_in_dim x2 -> x0, other arithmetic: 18.8 us -> none  [on_device(): jnp.where(match[:, :, None, None], kept[:, None], 0)]
    gather x24 -> x0, local copies, waits for them, and re-layouts: 11.3 us -> none
    dot_general x4 -> x0, matrix products: 8.49 us -> none  [the longest x2 7.85 us: tile_products(): jnp.einsum('tlik,tkc->tlic', tile_limbs, windows, preferred_element_type=...]
    all_to_all x2 -> x0, starting transfers between devices: 8.42 us -> none  [on_device(): lax.all_to_all(pieces, 'col', split_axis=0, concat_axis=0, tiled=True)]
  transfers between devices with their start and end apart: 2 -> 0, of which waited for: 1 -> 0; matrix products, arithmetic and copies ran while one was open for 2% -> 0% of each run, Pallas kernels for 0% -> 0%
where the time goes in v1:
time: 32.9 us; the launch traced here: 32.6 us
  Pallas kernels  28.6 us (87%)
  local copies, waits for them, and re-layouts  2.71 us (8%)
  between operations  1.31 us (4%)
    pallas_call x1, Pallas kernels, on_device(): pl.pallas_call(functools.partial(kernel, n_row, n_col), out_shape=jax.Sha...  28.6 us
    unnamed x1, local copies, waits for them, and re-layouts  1.38 us
    squeeze x1, local copies, waits for them, and re-layouts, on_device(): tile_index[0, 0]  1.34 us

profile of v1, /device:TPU:0, one launch (start us, length us, event | category | flops | bytes accessed | tf_op | source)
XLA Modules:
  0.0 32.6 jit_solution(13662281395667922190)
XLA Ops:
  1.3 1.3 %copy.8.index_ref = s32[4,2]{1,0:T(4,128)} copy(s32[4,2]{0,1:T(2,128)} %bitcast.9) | data formatting | bytes 64 | tf_op jit(solution)/shard_map/squeeze | solution.py:321
  2.6 28.6 %shard_map.73 = f32[32,256]{1,0:T(8,128)} custom-call(s32[4,2]{1,0:T(4,128)} %copy.8.index_ref, s32[1,1]{1,0:T(1,128)S(6)} %copy.10.count_ref, s32[1]{0:T(128)S(6)} %copy.11.degree_ref, f32[4,512,512]{2,1,0:T(8,128)} %bitcast.5, f32[32,256]{1,0:T(8,128)} %bitcast.7, f32[32,256]{1,0:T(8,128)} %bitcast.8, f32[8,32,32]{2,1,0:T(8,128)} %coef_ref.1), custom_call_target="tpu_custom_call" | custom-call | tf_op jit(solution)/shard_map/pallas_call | solution.py:287
  31.3 1.4 %copy.12 = f32[256,32]{0,1:T(8,128)} copy(f32[256,32]{0,1:T(8,128)} %bitcast.6) | data formatting | bytes 65536

commit v2 on v1

--- a/solution.py
+++ b/solution.py
@@ -46,14 +46,14 @@
 
 
 def kernel(
-    n_row, n_col, index_ref, count_ref, degree_ref, tiles_ref, iterate_ref, basis_ref, coef_ref,
-    out_ref, tbuf, abuf, gbuf, lbuf, wbuf, pbuf, rbuf, cur, bterm, csrc, crecv, fsum, frecv,
-    tile_sem, ag_send, ag_recv, rs_send, rs_recv, ca_send, ca_recv, cb_send, cb_recv,
+    n_row, n_col, index_hbm, count_ref, degree_ref, tiles_ref, iterate_hbm, basis_hbm, coef_hbm,
+    out_ref, iterate_ref, basis_ref, coef_ref, index_smem, tbuf, abuf, gbuf, lbuf, wbuf, pbuf, rbuf, cur, bterm, csrc, crecv, fsum, frecv,
+    small_sem, tile_sem, ag_send, ag_recv, af_send, rs_send, rs_recv, ca_send, ca_recv, cb_send, cb_recv,
 ):
     me_row = lax.axis_index("row")
     me_col = lax.axis_index("col")
     slots, tile, _ = tiles_ref.shape
-    width, rows_dev = iterate_ref.shape
+    width, rows_dev = iterate_hbm.shape
     per_tile = tile // rows_dev
     block_rows = n_col // per_tile
     band = RIGHT * width
@@ -61,9 +61,36 @@
     def row_peer(d):
         return lax.rem(me_row + d, n_row)
 
+    core = lax.rem(me_row, 2)
+    chip = lax.div(me_row, 2)
+    partner = me_row + 1 - 2 * core
+
+    def chip_peer(k, of_core):
+        index, bit = 0, 1
+        while bit < n_row // 2:
+            index = index + bit * lax.rem(lax.div(chip, bit) + k // bit % 2, 2)
+            bit *= 2
+        return 2 * index + of_core
+
+    far_first = range(n_row // 2 - 1, 0, -1)
+    near_first = sorted(range(1, n_row // 2), key=lambda k: bin(k).count("1"))
+
     def col_peer(d):
         return lax.rem(me_col + d, n_col)
 
+    small = [
+        pltpu.make_async_copy(src, dst, small_sem.at[i])
+        for i, (src, dst) in enumerate(
+            [
+                (iterate_hbm, iterate_ref),
+                (coef_hbm, coef_ref),
+                (index_hbm, index_smem),
+                (basis_hbm, basis_ref),
+            ]
+        )
+    ]
+    for load in small:
+        load.start()
     loads = [
         pltpu.make_async_copy(tiles_ref.at[t], tbuf.at[t], tile_sem.at[t]) for t in range(slots)
     ]
@@ -80,25 +107,38 @@
     def _(d):
         pl.semaphore_signal(barrier, inc=1, device_id={"col": col_peer(d)}, device_id_type=MESH)
 
-    per_device = coef_ref.shape[0]
+    per_device = coef_hbm.shape[0]
     me = me_row * n_col + me_col
+    small[1].wait()
     held = []
     for step in range(STEPS):
-        wanted = degree_ref[0] - step
-        matrix = coef_ref[lax.rem(wanted + per_device, per_device)]
-        matrix = jnp.where(lax.div(wanted, per_device) == me, matrix, 0.0)
+        wanted = jnp.broadcast_to(degree_ref[...] - step - me * per_device, (width, width))
+        matrix = jnp.where(wanted == 0, coef_ref[0], 0.0)
+        for k in range(1, per_device):
+            matrix = jnp.where(wanted == k, coef_ref[k], matrix)
         held += [matrix[: width // 2], matrix[width // 2 :]]
     csrc[...] = jnp.concatenate(held, axis=1)
 
+    small[0].wait()
     pl.semaphore_wait(barrier, n_row + n_col - 2)
 
-    def gather_copy(step, d, slot):
+    def gather_copy(step, peer, slot):
         return pltpu.make_async_remote_copy(
             src_ref=iterate_ref if step == 0 else cur,
             dst_ref=gbuf.at[step, slot],
-            send_sem=ag_send.at[step, d],
+            send_sem=ag_send.at[step, peer],
             recv_sem=ag_recv.at[step, slot],
-            device_id={"row": row_peer(d)},
+            device_id={"row": peer},
+            device_id_type=MESH,
+        )
+
+    def forward_copy(step, slot):
+        return pltpu.make_async_remote_copy(
+            src_ref=gbuf.at[step, slot],
+            dst_ref=gbuf.at[step, slot],
+            send_sem=af_send.at[step, slot],
+            recv_sem=ag_recv.at[step, slot],
+            device_id={"row": partner},
             device_id_type=MESH,
         )
 
@@ -149,6 +189,7 @@
                     abuf[place, at, t * tile : (t + 1) * tile] = parts[place].astype(jnp.bfloat16)
 
     def basis_terms():
+        small[3].wait()
         @pl.loop(1, n_row)
         def _(d):
             src = lax.rem(me_row - d + n_row, n_row)
@@ -184,9 +225,9 @@
             def _(d):
                 coef_col_copy(d, me_col).start()
 
-        @pl.loop(1, n_row)
-        def _(d, step=step):
-            gather_copy(step, d, me_row).start()
+        for k in far_first:
+            gather_copy(step, chip_peer(k, core), me_row).start()
+        gather_copy(step, partner, me_row).start()
 
         put_limbs((iterate_ref if step == 0 else cur)[...], me_row)
         if step == 0:
@@ -199,10 +240,13 @@
 
             fsum[...] = lax.fori_loop(1, n_col, add_col, csrc[...])
 
-        @pl.loop(1, n_row)
-        def _(d, step=step):
-            src = lax.rem(me_row - d + n_row, n_row)
-            gather_copy(step, d, src).wait_recv()
+        for k in near_first:
+            src = chip_peer(k, core)
+            gather_copy(step, src, src).wait_recv()
+            forward_copy(step, src).start()
+            put_limbs(gbuf[step, src], src)
+        for src in [partner] + [chip_peer(k, 1 - core) for k in near_first]:
+            gather_copy(step, partner, src).wait_recv()
             put_limbs(gbuf[step, src], src)
 
         if step == 0:
@@ -211,14 +255,17 @@
             def _(d):
                 coef_row_copy(d, me_row).start()
 
+        if step == 0:
+            small[2].wait()
+        count = jnp.max(count_ref[...])
         for t in range(slots):
-            column = index_ref[t, 1]
-            used = t < count_ref[0, 0]
+            used = t < count
+            column = index_smem[1, t]
             for part in range(per_tile):
                 window = lbuf[column * per_tile + part]
                 at = t * tile + part * rows_dev
                 for a in range(block_rows):
-                    keep = jnp.where(used & (index_ref[t, 0] == a), 1.0, 0.0).astype(jnp.bfloat16)
+                    keep = jnp.where(used & (index_smem[0, t] == a), 1.0, 0.0).astype(jnp.bfloat16)
                     wbuf[a * band : (a + 1) * band, at : at + rows_dev] = window * keep
 
         for part in range(per_tile):
@@ -263,10 +310,14 @@
             value = jnp.where(value < 0, value + PRIME, value)
             out_ref[...] = value.astype(jnp.float32) / float(PRIME)
 
+    for step in range(STEPS):
+        gather_copy(step, partner, me_row).wait_send()
+        for k in near_first:
+            gather_copy(step, chip_peer(k, core), me_row).wait_send()
+            forward_copy(step, chip_peer(k, core)).wait_send()
+
     @pl.loop(1, n_row)
     def _(d):
-        for step in range(STEPS):
-            gather_copy(step, d, me_row).wait_send()
         coef_row_copy(d, me_row).wait_send()
 
     @pl.loop(1, n_col)
@@ -287,11 +338,16 @@
     out = pl.pallas_call(
         functools.partial(kernel, n_row, n_col),
         out_shape=jax.ShapeDtypeStruct((width, rows_dev), f32),
-        in_specs=[pl.BlockSpec(memory_space=smem)] * 3
-        + [pl.BlockSpec(memory_space=pl.ANY)]
-        + [pl.BlockSpec(memory_space=vmem)] * 3,
+        in_specs=[
+            pl.BlockSpec(memory_space=space)
+            for space in (pl.ANY, vmem, vmem, pl.ANY, pl.ANY, pl.ANY, pl.ANY)
+        ],
         out_specs=pl.BlockSpec(memory_space=vmem),
         scratch_shapes=[
+            vmem((width, rows_dev), f32),
+            vmem((width, rows_dev), f32),
+            vmem(coefficients.shape, f32),
+            smem((2, slots), jnp.int32),
             vmem((slots, tile, tile), f32),
             vmem((LEFT, tile, slots * tile), bf16),
             vmem((STEPS, n_row, width, rows_dev), f32),
@@ -305,7 +361,9 @@
             vmem((n_col, width // 2, 2 * STEPS * width), f32),
             vmem((width // 2, 2 * STEPS * width), f32),
             vmem((n_row, width // 2, 2 * STEPS * width), f32),
+            dma((4,)),
             dma((slots,)),
+            dma((STEPS, n_row)),
             dma((STEPS, n_row)),
             dma((STEPS, n_row)),
             dma((STEPS, n_col)),
@@ -318,7 +376,7 @@
         compiler_params=pltpu.CompilerParams(
             collective_id=0, has_side_effects=True, vmem_limit_bytes=60 * 2**20
         ),
-    )(tile_index[0, 0], tile_count, start_degree, tiles[0, 0], iterate.T, basis.T, coefficients)
+    )(tile_index[0, 0].T, tile_count, start_degree.reshape(1, 1), tiles[0, 0], iterate.T, basis.T, coefficients)
     return out.T
 
 

time: 32.9 us -> 30.8 us (0.936)
  local copies, waits for them, and re-layouts: 2.71 us -> 1.38 us
  Pallas kernels: 28.6 us -> 27.9 us
    squeeze x1 -> x0, local copies, waits for them, and re-layouts: 1.34 us -> none  [on_device(): tile_index[0, 0]]
    pallas_call x1, Pallas kernels: 28.6 us -> 27.9 us  [on_device(): pl.pallas_call(functools.partial(kernel, n_row, n_col), out_shape=jax.Sha...]
where the time goes in v2:
time: 30.8 us; the launch traced here: 30.6 us
  Pallas kernels  27.9 us (91%)
  local copies, waits for them, and re-layouts  1.38 us (4%)
  between operations  1.3 us (4%)
    pallas_call x1, Pallas kernels, on_device(): pl.pallas_call(functools.partial(kernel, n_row, n_col), out_shape=jax.Sha...  27.9 us
    unnamed x1, local copies, waits for them, and re-layouts  1.38 us

profile of v2, /device:TPU:0, one launch (start us, length us, event | category | flops | bytes accessed | tf_op | source)
XLA Modules:
  0.0 30.6 jit_solution(1059827520495562271)
XLA Ops:
  1.3 27.9 %shard_map.73 = f32[32,256]{1,0:T(8,128)} custom-call(s32[2,4]{1,0:T(2,128)} %bitcast.13, s32[1,1]{1,0:T(1,128)S(6)} %copy.9.count_ref, s32[1,1]{1,0:T(1,128)} %bitcast.8.degree_ref, f32[4,512,512]{2,1,0:T(8,128)} %bitcast.9, f32[32,256]{1,0:T(8,128)} %bitcast.11, f32[32,256]{1,0:T(8,128)} %bitcast.12, f32[8,32,32]{2,1,0:T(8,128)} %coef_hbm.1), custom_call_target="tpu_custom_call" | custom-call | tf_op jit(solution)/shard_map/pallas_call | solution.py:338
  29.2 1.4 %copy.11 = f32[256,32]{0,1:T(8,128)} copy(f32[256,32]{0,1:T(8,128)} %bitcast.10) | data formatting | bytes 65536

commit v3 on v2

--- a/solution.py
+++ b/solution.py
@@ -47,8 +47,9 @@
 
 def kernel(
     n_row, n_col, index_hbm, count_ref, degree_ref, tiles_ref, iterate_hbm, basis_hbm, coef_hbm,
-    out_ref, iterate_ref, basis_ref, coef_ref, index_smem, tbuf, abuf, gbuf, lbuf, wbuf, pbuf, rbuf, cur, bterm, csrc, crecv, fsum, frecv,
-    small_sem, tile_sem, ag_send, ag_recv, af_send, rs_send, rs_recv, ca_send, ca_recv, cb_send, cb_recv,
+    out_ref, iterate_ref, basis_ref, coef_ref, index_smem, tbuf, abuf, gbuf, lbuf, wbuf, pbuf,
+    rbuf, cur, bterm, csrc, crecv, fsum, frecv, small_sem, tile_sem, ag_send, ag_recv, af_send,
+    rs_send, rs_recv, ca_send, ca_recv, cb_send, cb_recv,
 ):
     me_row = lax.axis_index("row")
     me_col = lax.axis_index("col")
@@ -337,7 +338,7 @@
     vmem, smem = pltpu.VMEM, pltpu.SMEM
     out = pl.pallas_call(
         functools.partial(kernel, n_row, n_col),
-        out_shape=jax.ShapeDtypeStruct((width, rows_dev), f32),
+        out_shape=vmem((width, rows_dev), f32),
         in_specs=[
             pl.BlockSpec(memory_space=space)
             for space in (pl.ANY, vmem, vmem, pl.ANY, pl.ANY, pl.ANY, pl.ANY)

time: 30.8 us -> 29.4 us (0.955)
  local copies, waits for them, and re-layouts: 1.38 us -> 0.62 us
  Pallas kernels: 27.9 us -> 27.3 us
    unnamed x1, local copies, waits for them, and re-layouts: 1.38 us -> 0.62 us
    pallas_call x1, Pallas kernels: 27.9 us -> 27.3 us  [on_device(): pl.pallas_call(functools.partial(kernel, n_row, n_col), out_shape=vmem((w...]
where the time goes in v3:
time: 29.4 us; the launch traced here: 29.2 us
  Pallas kernels  27.3 us (93%)
  between operations  1.3 us (4%)
  local copies, waits for them, and re-layouts  0.62 us (2%)
    pallas_call x1, Pallas kernels, on_device(): pl.pallas_call(functools.partial(kernel, n_row, n_col), out_shape=vmem((w...  27.3 us
    unnamed x1, local copies, waits for them, and re-layouts  0.62 us

profile of v3, /device:TPU:0, one launch (start us, length us, event | category | flops | bytes accessed | tf_op | source)
XLA Modules:
  0.0 29.2 jit_solution(14134693857591750917)
XLA Ops:
  1.3 27.3 %shard_map.73 = f32[32,256]{1,0:T(8,128)S(1)} custom-call(s32[2,4]{1,0:T(2,128)} %bitcast.13, s32[1,1]{1,0:T(1,128)S(6)} %copy.10.count_ref, s32[1,1]{1,0:T(1,128)} %bitcast.8.degree_ref, f32[4,512,512]{2,1,0:T(8,128)} %bitcast.10, f32[32,256]{1,0:T(8,128)} %bitcast.11, f32[32,256]{1,0:T(8,128)} %bitcast.12, f32[8,32,32]{2,1,0:T(8,128)} %coef_hbm.1), custom_call_target="tpu_custom_call" | custom-call | tf_op jit(solution)/shard_map/pallas_call | solution.py:339
  28.6 0.6 %copy.9 = f32[256,32]{0,1:T(8,128)} copy(f32[256,32]{0,1:T(8,128)S(1)} %bitcast.9) | data formatting | bytes 65536

commit v4 on v3

--- a/solution.py
+++ b/solution.py
@@ -234,13 +234,6 @@
         if step == 0:
             split_tiles()
 
-            def add_col(d, total):
-                src = lax.rem(me_col - d + n_col, n_col)
-                coef_col_copy(d, src).wait_recv()
-                return total + crecv[src]
-
-            fsum[...] = lax.fori_loop(1, n_col, add_col, csrc[...])
-
         for k in near_first:
             src = chip_peer(k, core)
             gather_copy(step, src, src).wait_recv()
@@ -251,6 +244,13 @@
             put_limbs(gbuf[step, src], src)
 
         if step == 0:
+
+            def add_col(d, total):
+                src = lax.rem(me_col - d + n_col, n_col)
+                coef_col_copy(d, src).wait_recv()
+                return total + crecv[src]
+
+            fsum[...] = lax.fori_loop(1, n_col, add_col, csrc[...])
 
             @pl.loop(1, n_row)
             def _(d):

time: 29.4 us -> 29.9 us (1.017)
  Pallas kernels: 27.3 us -> 27.8 us
    pallas_call x1, Pallas kernels: 27.3 us -> 27.8 us  [on_device(): pl.pallas_call(functools.partial(kernel, n_row, n_col), out_shape=vmem((w...]
where the time goes in v4:
time: 29.9 us; the launch traced here: 29.8 us
  Pallas kernels  27.8 us (93%)
  between operations  1.3 us (4%)
  local copies, waits for them, and re-layouts  0.62 us (2%)
    pallas_call x1, Pallas kernels, on_device(): pl.pallas_call(functools.partial(kernel, n_row, n_col), out_shape=vmem((w...  27.8 us
    unnamed x1, local copies, waits for them, and re-layouts  0.62 us

profile of v4, /device:TPU:0, one launch (start us, length us, event | category | flops | bytes accessed | tf_op | source)
XLA Modules:
  0.0 29.8 jit_solution(14255919998132570922)
XLA Ops:
  1.3 27.8 %shard_map.73 = f32[32,256]{1,0:T(8,128)S(1)} custom-call(s32[2,4]{1,0:T(2,128)} %bitcast.13, s32[1,1]{1,0:T(1,128)S(6)} %copy.10.count_ref, s32[1,1]{1,0:T(1,128)} %bitcast.8.degree_ref, f32[4,512,512]{2,1,0:T(8,128)} %bitcast.10, f32[32,256]{1,0:T(8,128)} %bitcast.11, f32[32,256]{1,0:T(8,128)} %bitcast.12, f32[8,32,32]{2,1,0:T(8,128)} %coef_hbm.1), custom_call_target="tpu_custom_call" | custom-call | tf_op jit(solution)/shard_map/pallas_call | solution.py:339
  29.1 0.6 %copy.9 = f32[256,32]{0,1:T(8,128)} copy(f32[256,32]{0,1:T(8,128)S(1)} %bitcast.9) | data formatting | bytes 65536
